TPU v7x, 32 devices: a whole 2x2x4 slice. The times are simulated.
32 devices in a mesh: feat: 8 (over y, x, core), rep: 4 (over z).
Axes of the slice: x: 2, y: 2, z: 4, core: 2. Of those that a mesh axis runs over, the one named last changes fastest.
Arguments:
- features: bfloat16 [4, 8, 1024, 512], P('rep', None, 'feat'), may hold values from -6 to 6
- adjacency_one: int32 [4, 8, 5, 16, 512], P('rep'), may hold values from 0 to 65535, as said below
- pre_hidden: bfloat16 [4, 8, 256, 256], P('rep', 'feat'), may hold values from -6 to 6
- adjacency_two: int32 [4, 8, 5, 8, 256], P('rep', 'feat'), may hold values from 0 to 65535, as said below
- weight_two: bfloat16 [6, 256, 256], replicated, may hold values from -0.375 to 0.375
- out_grad: bfloat16 [4, 8, 128, 256], P('rep', 'feat'), may hold values from -6 to 6
Outputs:
- grad_w1: float32 [6, 1024, 256], P(None, 'feat')
- grad_b1: float32 [256], replicated
- grad_w2: float32 [6, 256, 256], replicated
- grad_b2: float32 [256], replicated
Inputs may be any that keep to these rules, and one draw needn't show every extreme that they name: `adjacency_one`: bit k, k below 16, of word (w, n) is the entry of destination row 16 w + k and source column n; higher bits are zero; some rows are empty. `adjacency_two`: bit k, k below 16, of word (w, n) is the entry of seed row 16 w + k and source column n; higher bits are zero; some rows are empty.
All inputs are finite; a program needn't handle non-finite values.
Results may differ from a plain program's by a relative error of at most 0.0041.
Values may be sent and summed in bfloat16 or wider, within the bound.
No kernel may reach another device: no remote copies, remote signals or barrier semaphores. Data moves between devices by JAX's collectives and lax.ppermute only.
A program may use at most 128 MiB of HBM per device.

v0:
```python
import math
import jax
import jax.numpy as jnp
from jax import lax
from jax.sharding import PartitionSpec as P


def unpack(packed):
    shifts = jnp.arange(16, dtype=jnp.int32)
    spread = jnp.bitwise_and(jnp.right_shift(packed[..., None, :], shifts[:, None]), 1)
    dense = spread.reshape(packed.shape[:-2] + (packed.shape[-2] * 16, packed.shape[-1]))
    degree = jnp.sum(dense, axis=-1).astype(jnp.float32)
    return (dense.astype(jnp.bfloat16), 1.0 / jnp.maximum(degree, 1.0))


def upper_layer(pre_rows, words_two, grad_rows, weight_two, factor):
    hidden = jnp.maximum(pre_rows, 0)
    seed_count = grad_rows.shape[0]
    matrix, inverse = unpack(words_two)
    mixed = (
        jnp.einsum("rsd,dh->rsh", matrix, hidden, preferred_element_type=jnp.float32)
        * inverse[..., None]
    ).astype(jnp.bfloat16)
    scaled = grad_rows.astype(jnp.float32) * factor
    scaled_low = scaled.astype(jnp.bfloat16)
    grad_rel = jnp.einsum("rsh,sk->rhk", mixed, scaled_low, preferred_element_type=jnp.float32)
    grad_self = jnp.einsum(
        "sh,sk->hk", hidden[:seed_count], scaled_low, preferred_element_type=jnp.float32
    )
    weight_grad = jnp.concatenate([grad_self[None], grad_rel], 0)
    backed = (
        jnp.einsum("sk,rhk->rsh", scaled_low, weight_two[1:], preferred_element_type=jnp.float32)
        * inverse[..., None]
    ).astype(jnp.bfloat16)
    spread_back = jnp.einsum("rsd,rsh->dh", matrix, backed, preferred_element_type=jnp.float32)
    own_part = jnp.einsum(
        "sk,hk->sh", scaled_low, weight_two[0], preferred_element_type=jnp.float32
    )
    hidden_total = spread_back + jnp.pad(own_part, ((0, hidden.shape[0] - seed_count), (0, 0)))
    hidden_grad = jnp.where(pre_rows > 0, hidden_total, 0.0).astype(jnp.bfloat16)
    return (
        weight_grad,
        jnp.sum(scaled, 0),
        hidden_grad,
        jnp.sum(hidden_grad.astype(jnp.float32), 0),
    )


def panel_terms(word_block, column_block, grad_block):
    matrix, inverse = unpack(word_block)
    rows_one = grad_block.shape[1]
    gathered = (
        jnp.einsum("brdn,bcn->brdc", matrix, column_block, preferred_element_type=jnp.float32)
        * inverse[..., None]
    ).astype(jnp.bfloat16)
    panel_rel = jnp.einsum(
        "brdc,bdh->rch", gathered, grad_block, preferred_element_type=jnp.float32
    )
    panel_self = jnp.einsum(
        "bcd,bdh->ch", column_block[:, :, :rows_one], grad_block, preferred_element_type=jnp.float32
    )
    return jnp.concatenate([panel_self[None], panel_rel], 0)


def on_device(features, adjacency_one, pre_hidden, adjacency_two, weight_two, out_grad):
    seed_count = out_grad.shape[2]
    factor = float(seed_count * lax.axis_size("feat") * lax.axis_size("rep")) ** (-0.5)
    weight_grad, bias_two, hidden_grad, bias_one = upper_layer(
        pre_hidden[0, 0], adjacency_two[0, 0], out_grad[0, 0], weight_two, factor
    )
    feature_local = features[0]
    adj_local = adjacency_one[0]
    col_width = feature_local.shape[1]
    hidden_width = hidden_grad.shape[1]
    relations = adj_local.shape[1]
    initial = jnp.zeros((relations + 1, col_width, hidden_width), jnp.float32)
    piece = lax.all_gather(hidden_grad[None], "feat", axis=0, tiled=True)
    piece_rows = piece.shape[0]
    group_size = math.gcd(piece_rows, 8)
    turn_count = piece_rows // group_size
    word_block = adj_local
    word_block = word_block.reshape((turn_count, group_size) + adj_local.shape[1:])
    column_block = feature_local
    column_block = column_block.reshape((turn_count, group_size) + feature_local.shape[1:])
    grad_block = piece.reshape((turn_count, group_size) + piece.shape[1:])

    def one_turn(running, inputs):
        return (running + panel_terms(inputs[0], inputs[1], inputs[2]), None)

    running, unused = lax.scan(one_turn, initial, (word_block, column_block, grad_block))
    grad_w1 = lax.psum(running, "rep")
    grad_w2, grad_b1, grad_b2 = lax.psum((weight_grad, bias_one, bias_two), ("feat", "rep"))
    return (grad_w1, grad_b1, grad_w2, grad_b2)


def solution(mesh):
    placed = (
        P("rep", None, "feat", None),
        P("rep", None, None, None, None),
        P("rep", "feat", None, None),
        P("rep", "feat", None, None, None),
        P(),
        P("rep", "feat", None, None),
    )
    return jax.shard_map(
        on_device,
        mesh=mesh,
        in_specs=placed,
        out_specs=(P(None, "feat", None), P(), P(), P()),
        check_vma=False,
    )
```

profile of v0, /device:TPU:0, one launch (start us, length us, event | category | flops | bytes accessed | tf_op | source)
XLA Modules:
  0.0 213.1 jit_solution(5158156742498113044)
XLA Ops:
  8.0 0.0 copy-start
  8.0 0.0 all-gather.3.cloned.1.call-start
  8.1 1.6 fusion.28
  9.7 0.1 div.22
  9.8 0.1 shift_right_arithmetic.72
  9.9 0.9 fusion.27
  10.8 1.1 fusion.37
  11.9 2.4 %convert_reduce_fusion = (f32[256]{0:T(256)S(1)}, bf16[256,256]{1,0:T(8,128)(2,1)}) fusion(f32[128,256]{1,0:T(8,128)S(1)} %fusion.37, bf16[5,128,256]{2,1,0:T(8,128)(2,1)S(1)} %fusion.27, bf16[6,256,256]{2,1,0:T(8,128)(2,1)} %param.10, f32[5,128]{1,0:T(8,128)S(1)} %div.22, bf16[1,1,128,256]{3,2,1,0:T(8,128)(2,1)} %param.11, bf16[1,1,256,256]{3,2,1,0:T(8,128)(2,1)} %param.8), kind=kOutput, calls=%fused_computation.38 | convolution fusion | flops 168722176 | bytes 1445376 | tf_op jit(solution)/shard_map/rsd,rsh->dh/dot_general | solution.py:35
  14.4 0.0 all-gather.3.cloned.1.call-update
  14.4 0.0 all-reduce.7.cloned.1.call-start
  14.4 0.9 broadcast_maximum_fusion
  15.4 1.0 convolution_bitcast_fusion.1
  16.4 1.6 fusion.19
  18.0 1.2 pad_maximum_fusion
  19.3 0.0 all-reduce.7.cloned.1.call-update
  19.3 0.2 all-reduce.5.cloned.1.call-start
  19.5 0.0 copy-done
  19.5 10.9 %and_reduce_fusion = s32[8,5,16,16]{3,2,1,0:T(8,128)S(1)} fusion(s32[8,5,16,512]{3,2,1,0:T(8,128)S(1)} %bitcast.90), kind=kLoop, calls=%fused_computation.3 | loop fusion | flops 15718400 | bytes 1351680 | tf_op jit(solution)/shard_map/while/body/eval_jaxpr/reduce_sum | solution.py:12
  30.4 0.1 maximum_divide_fusion
  30.5 0.2 reshape.90
  30.7 0.1 shift_right_arithmetic.81
  30.7 10.1 %all-gather.3.cloned.1.call-done = bf16[2048,256]{1,0:T(8,128)(2,1)} async-done(((bf16[256,256]{1,0:T(8,128)(2,1)}), bf16[2048,256]{1,0:T(8,128)(2,1)}) %all-gather.3.cloned.1.call-update) | async-done | bytes 1048592 | tf_op jit(solution)/shard_map/all_gather | solution.py:77
  40.9 0.0 copy-start.2
  40.9 0.0 copy-start.3
  40.9 10.5 %shift_right_arithmetic.78 = s32[8,5,16,16,512]{4,3,2,1,0:T(8,128)} broadcast(s32[8,5,16,512]{3,2,1,0:T(8,128)S(1)} %bitcast.91), dimensions={0,1,2,4} | broadcast | bytes 22282240 | tf_op jit(solution)/shard_map/while/body/eval_jaxpr/shift_right_arithmetic | solution.py:10
  51.3 0.0 copy-done.2
  51.3 0.0 copy-done.3
  51.3 0.0 copy-start.1
  51.3 9.5 %fusion.13 = f32[5,128,256]{2,1,0:T(8,128)S(1)} fusion(bf16[8,256,256,1]{2,1,0,3:T(8,128)(2,1)S(1)} %bitcast.96, f32[8,5,256]{2,0,1:T(8,128)S(1)} %copy.37, s32[8,5,256,512]{3,2,1,0:T(8,128)} %bitcast.89, s32[256]{0:T(256)S(1)} %shift_right_arithmetic.81, bf16[1,8,128,512]{3,2,1,0:T(8,128)(2,1)S(1)} %copy-done.2), kind=kOutput, calls=%fused_computation.14 | convolution fusion | flops 2031616000 | bytes 23766016 | tf_op jit(solution)/shard_map/while/body/eval_jaxpr/brdc,bdh->rch/dot_general | solution.py:56
  60.8 0.5 convolution_bitcast_fusion.2
  61.3 0.1 copy.30
  61.4 1.0 pad_maximum_fusion.1
  62.4 0.0 all-reduce.5.cloned.1.call-update
  62.4 0.0 copy-done.1
  62.4 39.3 %all-reduce.1 = (f32[256]{0:T(256)}, f32[256]{0:T(256)}) all-reduce(f32[256]{0:T(256)S(1)} %get-tuple-element.23, f32[256]{0:T(256)S(1)} %fusion.40), channel_id=1, replica_groups=mesh['feat'=8,'rep'=4] {'feat','rep'}, use_global_device_ids=true, to_apply=%region_4.5 | all-reduce | flops 512 | bytes 4096 | tf_op jit(solution)/shard_map/psum | solution.py:92
  101.8 53.7 %all-reduce.7.cloned.1.call-done = f32[6,256,256]{2,1,0:T(8,128)} async-done(((f32[6,256,256]{2,1,0:T(8,128)}), f32[6,256,256]{2,1,0:T(8,128)}) %all-reduce.7.cloned.1.call-update) | async-done | bytes 1572880 | tf_op jit(solution)/shard_map/psum | solution.py:92
  155.4 45.4 %all-reduce.5.cloned.1.call-done = f32[6,128,256]{2,1,0:T(8,128)} async-done(((f32[6,128,256]{2,1,0:T(8,128)}), f32[6,128,256]{2,1,0:T(8,128)}) %all-reduce.5.cloned.1.call-update) | async-done | bytes 786448 | tf_op jit(solution)/shard_map/psum | solution.py:91
  200.8 2.1 copy.52
  202.9 2.7 %copy.53 = f32[6,256,256]{2,1,0:T(8,128)} copy(f32[6,256,256]{2,1,0:T(8,128)} %all-reduce.7.cloned.1.call-done) | data formatting | bytes 3145728
  (5 shorter events, 0.1 us)
Async XLA Ops:
  8.0 11.5 %copy-start = (s32[1,8,5,16,512]{4,3,2,1,0:T(8,128)S(1)}, s32[1,8,5,16,512]{4,3,2,1,0:T(8,128)}, u32[]{:S(2)}) copy-start(s32[1,8,5,16,512]{4,3,2,1,0:T(8,128)} %param.7) | copy-start | bytes 3932164
  8.0 32.9 %all-gather.3.cloned.1.call-start = ((), (), s32[]{:S(2)}) async-start(), calls=%async_computation.2 | async-start | bytes 1179648 | tf_op jit(solution)/shard_map/all_gather | solution.py:77
  14.4 141.0 %all-reduce.7.cloned.1.call-start = ((), (), s32[]{:S(2)}) async-start(), calls=%async_computation.1 | async-start | bytes 3145728 | tf_op jit(solution)/shard_map/psum | solution.py:92
  19.3 181.5 %all-reduce.5.cloned.1.call-start = ((), (), s32[]{:S(2)}) async-start(), calls=%async_computation | async-start | bytes 1572864 | tf_op jit(solution)/shard_map/psum | solution.py:91
  40.9 10.5 %copy-start.2 = (bf16[1,8,128,512]{3,2,1,0:T(8,128)(2,1)S(1)}, bf16[1,8,128,512]{3,2,1,0:T(8,128)(2,1)}, u32[]{:S(2)}) copy-start(bf16[1,8,128,512]{3,2,1,0:T(8,128)(2,1)} %param.6) | copy-start | bytes 3145732
  40.9 10.5 %copy-start.3 = (bf16[2048,256]{1,0:T(8,128)(2,1)S(1)}, bf16[2048,256]{1,0:T(8,128)(2,1)}, u32[]{:S(2)}) copy-start(bf16[2048,256]{1,0:T(8,128)(2,1)} %all-gather.3.cloned.1.call-done) | copy-start | bytes 3145732
  51.3 11.0 %copy-start.1 = (bf16[1,1,128,256]{3,2,1,0:T(8,128)(2,1)S(1)}, bf16[1,1,128,256]{3,2,1,0:T(8,128)(2,1)}, u32[]{:S(2)}) copy-start(bf16[1,1,128,256]{3,2,1,0:T(8,128)(2,1)} %param.11) | copy-start | bytes 196612
Sparse Core Ops, SparseCore 0:
  14.5 26.3 all-gather.2
Sparse Core Ops, SparseCore 1:
  20.7 134.6 all-reduce.6
  158.2 42.5 all-reduce.4
where the time goes:
time: 214 us; the launch traced here: 213 us
  waiting for transfers between devices  109 us (51%)
  blocking collectives  39.3 us (18%)
  other arithmetic  16.6 us (8%)
  matrix products  16.1 us (8%)
  local copies, waits for them, and re-layouts  15.8 us (7%)
  between operations  15.6 us (7%)
    psum x1, waiting for transfers between devices, on_device(): lax.psum((weight_grad, bias_one, bias_two), ('feat', 'rep'))  53.7 us
    psum x1, waiting for transfers between devices, on_device(): grad_w1 = lax.psum(running, 'rep')  45.4 us
    psum x1, blocking collectives, on_device(): lax.psum((weight_grad, bias_one, bias_two), ('feat', 'rep'))  39.3 us
    reduce_sum x1, other arithmetic, unpack(): degree = jnp.sum(dense, axis=-1).astype(jnp.float32)  10.9 us
    shift_right_arithmetic x5, local copies, waits for them, and re-layouts, unpack(): jnp.right_shift(packed[..., None, :], shifts[:, None])  10.6 us
    all_gather x1, waiting for transfers between devices, on_device(): piece = lax.all_gather(hidden_grad[None], 'feat', axis=0, tiled=True)  10.1 us
    dot_general x1, matrix products, panel_terms(): jnp.einsum('brdc,bdh->rch', gathered, grad_block, preferred_element_type=...  9.46 us
    unnamed x10, local copies, waits for them, and re-layouts  4.85 us
  transfers between devices with their start and end apart: 3, of which 3 were waited for; matrix products, arithmetic and copies ran while one was open for 18% of the time, Pallas kernels for 0%

commit v1 on v0

--- a/solution.py
+++ b/solution.py
@@ -89,7 +89,7 @@
 
     running, unused = lax.scan(one_turn, initial, (word_block, column_block, grad_block))
     grad_w1 = lax.psum(running, "rep")
-    grad_w2, grad_b1, grad_b2 = lax.psum((weight_grad, bias_one, bias_two), ("feat", "rep"))
+    grad_w2, grad_b1, grad_b2 = lax.psum(lax.psum((weight_grad, bias_one, bias_two), "feat"), "rep")
     return (grad_w1, grad_b1, grad_w2, grad_b2)
 
 

time: 214 us -> 212 us (level)
  waiting for transfers between devices: 109 us -> 124 us
  blocking collectives: 39.3 us -> 24.9 us
    psum x1, waiting for transfers between devices: 45.4 us -> 72.4 us  [on_device(): grad_w1 = lax.psum(running, 'rep')]
    psum x1 -> x2, blocking collectives: 39.3 us -> 24.9 us  [the longest x1 13.1 us: on_device(): lax.psum(lax.psum((weight_grad, bias_one, bias_two), 'feat'), 'rep')]
    psum x1, waiting for transfers between devices: 53.7 us -> 41.6 us  [on_device(): lax.psum((weight_grad, bias_one, bias_two), 'feat')]
where the time goes in v1:
time: 212 us; the launch traced here: 211 us
  waiting for transfers between devices  124 us (58%)
  blocking collectives  24.9 us (12%)
  other arithmetic  16.7 us (8%)
  matrix products  16.1 us (8%)
  local copies, waits for them, and re-layouts  15.5 us (7%)
  between operations  13.9 us (7%)
    psum x1, waiting for transfers between devices, on_device(): grad_w1 = lax.psum(running, 'rep')  72.4 us
    psum x1, waiting for transfers between devices, on_device(): lax.psum((weight_grad, bias_one, bias_two), 'feat')  41.6 us
    psum x1, blocking collectives, on_device(): lax.psum(lax.psum((weight_grad, bias_one, bias_two), 'feat'), 'rep')  13.1 us
    psum x1, blocking collectives, on_device(): lax.psum((weight_grad, bias_one, bias_two), 'feat')  11.8 us
    reduce_sum x1, other arithmetic, unpack(): degree = jnp.sum(dense, axis=-1).astype(jnp.float32)  10.9 us
    shift_right_arithmetic x5, local copies, waits for them, and re-layouts, unpack(): jnp.right_shift(packed[..., None, :], shifts[:, None])  10.3 us
    all_gather x1, waiting for transfers between devices, on_device(): piece = lax.all_gather(hidden_grad[None], 'feat', axis=0, tiled=True)  9.83 us
    dot_general x1, matrix products, panel_terms(): jnp.einsum('brdc,bdh->rch', gathered, grad_block, preferred_element_type=...  9.39 us
  transfers between devices with their start and end apart: 3, of which 3 were waited for; matrix products, arithmetic and copies ran while one was open for 18% of the time, Pallas kernels for 0%

profile of v1, /device:TPU:0, one launch (start us, length us, event | category | flops | bytes accessed | tf_op | source)
XLA Modules:
  0.0 211.1 jit_solution(1814039624088540811)
XLA Ops:
  7.2 0.0 all-gather.3.cloned.1.call-start
  7.2 0.0 copy-start
  7.2 1.6 fusion.28
  8.9 0.1 div.22
  9.0 0.1 shift_right_arithmetic.72
  9.0 0.9 fusion.27
  10.0 1.1 fusion.37
  11.1 2.4 %convert_reduce_fusion = (f32[256]{0:T(256)S(1)}, bf16[256,256]{1,0:T(8,128)(2,1)}) fusion(f32[128,256]{1,0:T(8,128)S(1)} %fusion.37, bf16[5,128,256]{2,1,0:T(8,128)(2,1)S(1)} %fusion.27, bf16[6,256,256]{2,1,0:T(8,128)(2,1)} %param.10, f32[5,128]{1,0:T(8,128)S(1)} %div.22, bf16[1,1,128,256]{3,2,1,0:T(8,128)(2,1)} %param.11, bf16[1,1,256,256]{3,2,1,0:T(8,128)(2,1)} %param.8), kind=kOutput, calls=%fused_computation.38 | convolution fusion | flops 168722176 | bytes 1445376 | tf_op jit(solution)/shard_map/rsd,rsh->dh/dot_general | solution.py:35
  13.5 0.0 all-gather.3.cloned.1.call-update
  13.6 0.0 all-reduce.7.cloned.1.call-start
  13.6 0.9 broadcast_maximum_fusion
  14.5 1.0 convolution_bitcast_fusion.1
  15.6 1.6 fusion.19
  17.2 1.3 pad_maximum_fusion
  18.5 0.0 all-reduce.7.cloned.1.call-update
  18.5 0.2 all-reduce.9.cloned.1.call-start
  18.8 0.0 copy-done
  18.8 10.9 %and_reduce_fusion = s32[8,5,16,16]{3,2,1,0:T(8,128)S(1)} fusion(s32[8,5,16,512]{3,2,1,0:T(8,128)S(1)} %bitcast.90), kind=kLoop, calls=%fused_computation.3 | loop fusion | flops 15718400 | bytes 1351680 | tf_op jit(solution)/shard_map/while/body/eval_jaxpr/reduce_sum | solution.py:12
  29.6 0.1 maximum_divide_fusion
  29.7 0.2 reshape.90
  29.9 0.1 shift_right_arithmetic.81
  30.0 9.8 %all-gather.3.cloned.1.call-done = bf16[2048,256]{1,0:T(8,128)(2,1)} async-done(((bf16[256,256]{1,0:T(8,128)(2,1)}), bf16[2048,256]{1,0:T(8,128)(2,1)}) %all-gather.3.cloned.1.call-update) | async-done | bytes 1048592 | tf_op jit(solution)/shard_map/all_gather | solution.py:77
  39.8 0.0 copy-start.2
  39.8 0.0 copy-start.3
  39.8 10.1 %shift_right_arithmetic.78 = s32[8,5,16,16,512]{4,3,2,1,0:T(8,128)} broadcast(s32[8,5,16,512]{3,2,1,0:T(8,128)S(1)} %bitcast.91), dimensions={0,1,2,4} | broadcast | bytes 22282240 | tf_op jit(solution)/shard_map/while/body/eval_jaxpr/shift_right_arithmetic | solution.py:10
  49.9 0.0 copy-done.2
  50.0 0.0 copy-done.3
  50.0 9.4 %fusion.13 = f32[5,128,256]{2,1,0:T(8,128)S(1)} fusion(bf16[8,256,256,1]{2,1,0,3:T(8,128)(2,1)S(1)} %bitcast.96, f32[8,5,256]{2,0,1:T(8,128)S(1)} %copy.37, s32[8,5,256,512]{3,2,1,0:T(8,128)} %bitcast.89, s32[256]{0:T(256)S(1)} %shift_right_arithmetic.81, bf16[1,8,128,512]{3,2,1,0:T(8,128)(2,1)S(1)} %copy-done.2), kind=kOutput, calls=%fused_computation.14 | convolution fusion | flops 2031616000 | bytes 23766016 | tf_op jit(solution)/shard_map/while/body/eval_jaxpr/brdc,bdh->rch/dot_general | solution.py:56
  59.4 0.0 copy-start.1
  59.4 0.5 convolution_bitcast_fusion.2
  59.8 0.1 copy.30
  59.9 0.9 pad_maximum_fusion.1
  60.9 41.6 %all-reduce.7.cloned.1.call-done = f32[6,256,256]{2,1,0:T(8,128)} async-done(((f32[6,256,256]{2,1,0:T(8,128)}), f32[6,256,256]{2,1,0:T(8,128)}) %all-reduce.7.cloned.1.call-update) | async-done | bytes 1572880 | tf_op jit(solution)/shard_map/psum | solution.py:92
  102.5 0.0 all-reduce.9.cloned.1.call-update
  102.5 0.0 copy-done.1
  102.5 11.8 %all-reduce.1 = (f32[256]{0:T(256)S(1)}, f32[256]{0:T(256)S(1)}) all-reduce(f32[256]{0:T(256)S(1)} %get-tuple-element.27, f32[256]{0:T(256)S(1)} %fusion.40), channel_id=1, replica_groups=mesh['feat'=8,'rep'=4] {'feat'}, use_global_device_ids=true, to_apply=%region_4.5 | all-reduce | flops 512 | bytes 4096 | tf_op jit(solution)/shard_map/psum | solution.py:92
  114.3 13.1 %all-reduce.2 = (f32[256]{0:T(256)}, f32[256]{0:T(256)}) all-reduce(f32[256]{0:T(256)S(1)} %get-tuple-element.14, f32[256]{0:T(256)S(1)} %get-tuple-element.20), channel_id=1, replica_groups=mesh['feat'=8,'rep'=4] {'rep'}, use_global_device_ids=true, to_apply=%region_5.6 | all-reduce | flops 512 | bytes 4096 | tf_op jit(solution)/shard_map/psum | solution.py:92
  127.4 72.4 %all-reduce.9.cloned.1.call-done = (f32[6,128,256]{2,1,0:T(8,128)}, f32[6,256,256]{2,1,0:T(8,128)}) async-done(((f32[6,128,256]{2,1,0:T(8,128)}, f32[6,256,256]{2,1,0:T(8,128)}), (f32[6,128,256]{2,1,0:T(8,128)}, f32[6,256,256]{2,1,0:T(8,128)})) %all-reduce.9.cloned.1.call-update) | async-done | bytes 2359312 | tf_op jit(solution)/shard_map/psum | solution.py:91
  199.8 2.1 copy.53
  201.9 2.7 %copy.54 = f32[6,256,256]{2,1,0:T(8,128)} copy(f32[6,256,256]{2,1,0:T(8,128)} %get-tuple-element.31) | data formatting | bytes 3145728
  (5 shorter events, 0.1 us)
Async XLA Ops:
  7.2 32.7 %all-gather.3.cloned.1.call-start = ((), (), s32[]{:S(2)}) async-start(), calls=%async_computation.1 | async-start | bytes 1179648 | tf_op jit(solution)/shard_map/all_gather | solution.py:77
  7.2 11.6 %copy-start = (s32[1,8,5,16,512]{4,3,2,1,0:T(8,128)S(1)}, s32[1,8,5,16,512]{4,3,2,1,0:T(8,128)}, u32[]{:S(2)}) copy-start(s32[1,8,5,16,512]{4,3,2,1,0:T(8,128)} %param.7) | copy-start | bytes 3932164
  13.6 88.9 %all-reduce.7.cloned.1.call-start = ((), (), s32[]{:S(2)}) async-start(), calls=%async_computation | async-start | bytes 3145728 | tf_op jit(solution)/shard_map/psum | solution.py:92
  18.5 181.2 %all-reduce.9.cloned.1.call-start = ((), (), s32[]{:S(2)}) async-start(), calls=%async_computation.2 | async-start | bytes 4718592 | tf_op jit(solution)/shard_map/psum | solution.py:91
  39.8 10.1 %copy-start.2 = (bf16[1,8,128,512]{3,2,1,0:T(8,128)(2,1)S(1)}, bf16[1,8,128,512]{3,2,1,0:T(8,128)(2,1)}, u32[]{:S(2)}) copy-start(bf16[1,8,128,512]{3,2,1,0:T(8,128)(2,1)} %param.6) | copy-start | bytes 3145732
  39.8 10.1 %copy-start.3 = (bf16[2048,256]{1,0:T(8,128)(2,1)S(1)}, bf16[2048,256]{1,0:T(8,128)(2,1)}, u32[]{:S(2)}) copy-start(bf16[2048,256]{1,0:T(8,128)(2,1)} %all-gather.3.cloned.1.call-done) | copy-start | bytes 3145732
  59.4 43.1 %copy-start.1 = (bf16[1,1,128,256]{3,2,1,0:T(8,128)(2,1)S(1)}, bf16[1,1,128,256]{3,2,1,0:T(8,128)(2,1)}, u32[]{:S(2)}) copy-start(bf16[1,1,128,256]{3,2,1,0:T(8,128)(2,1)} %param.11) | copy-start | bytes 196612
Sparse Core Ops, SparseCore 0:
  13.7 26.0 all-gather.2
  43.6 58.7 all-reduce.6
  105.5 94.2 all-reduce.8
